TPU v7x, 32 devices: a whole 2x2x4 slice. The times are simulated.
32 devices in a mesh: group: 4 (over y, core), replica: 8 (over z, x).
Axes of the slice: x: 2, y: 2, z: 4, core: 2. Of those that a mesh axis runs over, the one named last changes fastest.
Arguments:
- inputs: bfloat16 [32, 128, 1600], P(('group', 'replica')), may hold values from -6 to 6
- segments: int32 [32, 128], P(('group', 'replica')), may hold values from 0 to 3, never falling along the last dimension, each value on 1 to 64 neighbouring positions
- cotangent: bfloat16 [32, 128, 1600], P(('group', 'replica')), may hold values from -6 to 6
- norm1_gain: bfloat16 [1600], P('group'), may hold values from 0.5 to 1.5
- norm1_bias: bfloat16 [1600], P('group'), may hold values from -3 to 3
- w_qkv: bfloat16 [1600, 4800], P('group'), may hold values from -8 to 8
- bias_qv: bfloat16 [3200], P('group'), may hold values from -3 to 3
- w_out: bfloat16 [1600, 1600], P('group'), may hold values from -0.625 to 0.625
- bias_out: bfloat16 [1600], P('group'), may hold values from -3 to 3
- norm2_gain: bfloat16 [1600], P('group'), may hold values from 0.5 to 1.5
- norm2_bias: bfloat16 [1600], P('group'), may hold values from -3 to 3
- w_fc: bfloat16 [1600, 6400], P('group'), may hold values from -0.15625 to 0.15625
- bias_fc: bfloat16 [6400], P('group'), may hold values from -3 to 3
- w_proj: bfloat16 [6400, 1600], P('group'), may hold values from -0.078125 to 0.078125
- bias_proj: bfloat16 [1600], P('group'), may hold values from -3 to 3
Outputs:
- outputs: bfloat16 [32, 128, 1600], P(('group', 'replica'))
- input_grad: float32 [32, 128, 1600], P(('group', 'replica'))
- grad_norm1_gain: float32 [1600], P('group')
- grad_norm1_bias: float32 [1600], P('group')
- grad_w_qkv: float32 [1600, 4800], P('group')
- grad_bias_qv: float32 [3200], P('group')
- grad_w_out: float32 [1600, 1600], P('group')
- grad_bias_out: float32 [1600], P('group')
- grad_norm2_gain: float32 [1600], P('group')
- grad_norm2_bias: float32 [1600], P('group')
- grad_w_fc: float32 [1600, 6400], P('group')
- grad_bias_fc: float32 [6400], P('group')
- grad_w_proj: float32 [6400, 1600], P('group')
- grad_bias_proj: float32 [1600], P('group')
Inputs may be any that keep to these rules, and one draw needn't show every extreme that they name: `segments`: each packed row's segment numbers never fall; a segment holds 1 to 64 tokens, and some segment holds exactly that many.
All inputs are finite; a program needn't handle non-finite values.
Results may differ from a plain program's by a relative error of at most 0.0095.
Values may be sent and summed in bfloat16 or wider, within the bound.
A program may use at most 640 MiB of HBM per device.

v0:
```python
import jax
import jax.numpy as jnp
from jax import lax
from jax.sharding import PartitionSpec as P

HEAD_DIM = 64
EPSILON = 1e-05
GELU_SCALE = 0.7978845608028654
CUBIC_TERM = 0.044715


def matmul_plain(left_side, right_side):
    return jnp.dot(left_side, right_side, preferred_element_type=jnp.float32)


def matmul_left(left_side, right_side):
    return lax.dot_general(
        left_side, right_side, (((0,), (0,)), ((), ())), preferred_element_type=jnp.float32
    )


def matmul_right(left_side, right_side):
    return lax.dot_general(
        left_side, right_side, (((1,), (1,)), ((), ())), preferred_element_type=jnp.float32
    )


def batched(form, left_side, right_side):
    return jnp.einsum(form, left_side, right_side, preferred_element_type=jnp.float32)


def norm_forward(values, norm_gain, offset):
    center = values - jnp.mean(values, axis=-1, keepdims=True)
    inverse = lax.rsqrt(jnp.mean(center * center, axis=-1, keepdims=True) + EPSILON)
    scaled = center * inverse
    return (scaled * norm_gain + offset, scaled, inverse)


def norm_backward(upstream, scaled, inverse, norm_gain):
    weighted = upstream * norm_gain
    result = inverse * (
        weighted
        - jnp.mean(weighted, axis=-1, keepdims=True)
        - scaled * jnp.mean(weighted * scaled, axis=-1, keepdims=True)
    )
    return (result, jnp.sum(upstream * scaled, axis=0), jnp.sum(upstream, axis=0))


def gelu_tanh(values):
    tangent = jnp.tanh(GELU_SCALE * (values + CUBIC_TERM * values * values * values))
    return 0.5 * values * (1.0 + tangent)


def gelu_slope(values):
    tangent = jnp.tanh(GELU_SCALE * (values + CUBIC_TERM * values * values * values))
    return 0.5 * (1.0 + tangent) + 0.5 * values * (1.0 - tangent * tangent) * GELU_SCALE * (
        1.0 + 3.0 * CUBIC_TERM * values * values
    )


def allowed_mask(segments):
    positions = jnp.arange(segments.shape[1])
    causal = positions[:, None] >= positions[None, :]
    same_segment = segments[:, :, None] == segments[:, None, :]
    return (same_segment & causal[None, :, :])[:, None, :, :]


def masked_scores(queries, keyed, allowed):
    raw = batched("rqhd,rkhd->rhqk", queries, keyed) * HEAD_DIM ** (-0.5)
    return jnp.where(allowed, raw, -1e30)


def layer_forward(inputs, segments, params):
    (
        norm1_gain,
        norm1_bias,
        w_qkv,
        bias_qv,
        w_out,
        bias_out,
        norm2_gain,
        norm2_bias,
        w_fc,
        bias_fc,
        w_proj,
        bias_proj,
    ) = params
    row_count, length, feature_width = inputs.shape
    head_count = feature_width // HEAD_DIM
    tokens = inputs.reshape(row_count * length, feature_width).astype(jnp.float32)
    first_norm, first_scaled, first_inverse = norm_forward(
        tokens, norm1_gain.astype(jnp.float32), norm1_bias.astype(jnp.float32)
    )
    first_cast = first_norm.astype(jnp.bfloat16)
    qkv_bias = jnp.concatenate(
        [
            bias_qv[:feature_width].astype(jnp.float32),
            jnp.zeros((feature_width,), jnp.float32),
            bias_qv[feature_width:].astype(jnp.float32),
        ]
    )
    projected = (matmul_plain(first_cast, w_qkv) + qkv_bias).astype(jnp.bfloat16)
    split_qkv = projected.reshape(row_count, length, 3, head_count, HEAD_DIM)
    queries, keyed, values = (split_qkv[:, :, 0], split_qkv[:, :, 1], split_qkv[:, :, 2])
    allowed = allowed_mask(segments)
    scores = masked_scores(queries, keyed, allowed)
    row_peak = jnp.max(scores, axis=-1, keepdims=True)
    logsum = row_peak + jnp.log(jnp.sum(jnp.exp(scores - row_peak), axis=-1, keepdims=True))
    attn_probs = jnp.exp(scores - logsum).astype(jnp.bfloat16)
    attended = batched("rhqk,rkhd->rqhd", attn_probs, values).reshape(
        row_count * length, feature_width
    )
    attended_cast = attended.astype(jnp.bfloat16)
    residual = tokens + matmul_plain(attended_cast, w_out) + bias_out.astype(jnp.float32)
    second_norm, second_scaled, second_inverse = norm_forward(
        residual, norm2_gain.astype(jnp.float32), norm2_bias.astype(jnp.float32)
    )
    second_cast = second_norm.astype(jnp.bfloat16)
    hidden_pre = matmul_plain(second_cast, w_fc) + bias_fc.astype(jnp.float32)
    hidden = gelu_tanh(hidden_pre).astype(jnp.bfloat16)
    result = residual + matmul_plain(hidden, w_proj) + bias_proj.astype(jnp.float32)
    outputs = result.astype(jnp.bfloat16).reshape(row_count, length, feature_width)
    stored = (
        first_scaled,
        first_inverse,
        first_cast,
        projected,
        logsum,
        attended,
        attended_cast,
        second_scaled,
        second_inverse,
        second_cast,
        hidden_pre,
        hidden,
        allowed,
    )
    return (outputs, stored)


def layer_backward(cotangent, params, stored):
    (
        norm1_gain,
        norm1_bias,
        w_qkv,
        bias_qv,
        w_out,
        bias_out,
        norm2_gain,
        norm2_bias,
        w_fc,
        bias_fc,
        w_proj,
        bias_proj,
    ) = params
    (
        first_scaled,
        first_inverse,
        first_cast,
        projected,
        logsum,
        attended,
        attended_cast,
        second_scaled,
        second_inverse,
        second_cast,
        hidden_pre,
        hidden,
        allowed,
    ) = stored
    row_count, length, feature_width = cotangent.shape
    head_count = feature_width // HEAD_DIM
    token_count = row_count * length
    upstream_cast = cotangent.reshape(token_count, feature_width)
    upstream = upstream_cast.astype(jnp.float32)
    grad_w_proj = matmul_left(hidden, upstream_cast)
    grad_bias_proj = jnp.sum(upstream, axis=0)
    grad_hidden = matmul_right(upstream_cast, w_proj) * gelu_slope(hidden_pre)
    grad_hidden_cast = grad_hidden.astype(jnp.bfloat16)
    grad_w_fc = matmul_left(second_cast, grad_hidden_cast)
    grad_bias_fc = jnp.sum(grad_hidden, axis=0)
    second_back, grad_norm2_gain, grad_norm2_bias = norm_backward(
        matmul_right(grad_hidden_cast, w_fc),
        second_scaled,
        second_inverse,
        norm2_gain.astype(jnp.float32),
    )
    grad_residual = upstream + second_back
    grad_residual_cast = grad_residual.astype(jnp.bfloat16)
    grad_w_out = matmul_left(attended_cast, grad_residual_cast)
    grad_bias_out = jnp.sum(grad_residual, axis=0)
    grad_attended = (
        matmul_right(grad_residual_cast, w_out)
        .astype(jnp.bfloat16)
        .reshape(row_count, length, head_count, HEAD_DIM)
    )
    split_qkv = projected.reshape(row_count, length, 3, head_count, HEAD_DIM)
    queries, keyed, values = (split_qkv[:, :, 0], split_qkv[:, :, 1], split_qkv[:, :, 2])
    scores = masked_scores(queries, keyed, allowed)
    exact_probs = jnp.exp(scores - logsum)
    attn_probs = exact_probs.astype(jnp.bfloat16)
    grad_probs = batched("rqhd,rkhd->rhqk", grad_attended, values)
    row_delta = jnp.sum(
        grad_attended.astype(jnp.float32)
        * attended.reshape(row_count, length, head_count, HEAD_DIM),
        axis=-1,
    )
    row_delta = jnp.transpose(row_delta, (0, 2, 1))[:, :, :, None]
    grad_scores = (exact_probs * (grad_probs - row_delta) * HEAD_DIM ** (-0.5)).astype(jnp.bfloat16)
    grad_queries = batched("rhqk,rkhd->rqhd", grad_scores, keyed)
    grad_keyed = batched("rhqk,rqhd->rkhd", grad_scores, queries)
    grad_values = batched("rhqk,rqhd->rkhd", attn_probs, grad_attended)
    grad_projected = jnp.stack([grad_queries, grad_keyed, grad_values], axis=2).reshape(
        token_count, 3 * feature_width
    )
    grad_bias_qv = jnp.concatenate(
        [
            jnp.sum(grad_projected[:, :feature_width], axis=0),
            jnp.sum(grad_projected[:, 2 * feature_width :], axis=0),
        ]
    )
    grad_projected_cast = grad_projected.astype(jnp.bfloat16)
    grad_w_qkv = matmul_left(first_cast, grad_projected_cast)
    first_back, grad_norm1_gain, grad_norm1_bias = norm_backward(
        matmul_right(grad_projected_cast, w_qkv),
        first_scaled,
        first_inverse,
        norm1_gain.astype(jnp.float32),
    )
    input_grad = (grad_residual + first_back).reshape(row_count, length, feature_width)
    grads = (
        grad_norm1_gain,
        grad_norm1_bias,
        grad_w_qkv,
        grad_bias_qv,
        grad_w_out,
        grad_bias_out,
        grad_norm2_gain,
        grad_norm2_bias,
        grad_w_fc,
        grad_bias_fc,
        grad_w_proj,
        grad_bias_proj,
    )
    return (input_grad, grads)


def per_device(
    inputs,
    segments,
    cotangent,
    norm1_gain,
    norm1_bias,
    w_qkv,
    bias_qv,
    w_out,
    bias_out,
    norm2_gain,
    norm2_bias,
    w_fc,
    bias_fc,
    w_proj,
    bias_proj,
):
    forward_params = (
        lax.all_gather(norm1_gain, "group", axis=0, tiled=True),
        lax.all_gather(norm1_bias, "group", axis=0, tiled=True),
        lax.all_gather(w_qkv, "group", axis=0, tiled=True),
        lax.all_gather(bias_qv, "group", axis=0, tiled=True),
        lax.all_gather(w_out, "group", axis=0, tiled=True),
        lax.all_gather(bias_out, "group", axis=0, tiled=True),
        lax.all_gather(norm2_gain, "group", axis=0, tiled=True),
        lax.all_gather(norm2_bias, "group", axis=0, tiled=True),
        lax.all_gather(w_fc, "group", axis=0, tiled=True),
        lax.all_gather(bias_fc, "group", axis=0, tiled=True),
        lax.all_gather(w_proj, "group", axis=0, tiled=True),
        lax.all_gather(bias_proj, "group", axis=0, tiled=True),
    )
    outputs, stored = layer_forward(inputs, segments, forward_params)
    backward_params = (
        lax.all_gather(norm1_gain, "group", axis=0, tiled=True),
        lax.all_gather(norm1_bias, "group", axis=0, tiled=True),
        lax.all_gather(w_qkv, "group", axis=0, tiled=True),
        lax.all_gather(bias_qv, "group", axis=0, tiled=True),
        lax.all_gather(w_out, "group", axis=0, tiled=True),
        lax.all_gather(bias_out, "group", axis=0, tiled=True),
        lax.all_gather(norm2_gain, "group", axis=0, tiled=True),
        lax.all_gather(norm2_bias, "group", axis=0, tiled=True),
        lax.all_gather(w_fc, "group", axis=0, tiled=True),
        lax.all_gather(bias_fc, "group", axis=0, tiled=True),
        lax.all_gather(w_proj, "group", axis=0, tiled=True),
        lax.all_gather(bias_proj, "group", axis=0, tiled=True),
    )
    input_grad, grads = layer_backward(cotangent, backward_params, stored)
    owned = (
        lax.psum_scatter(grads[0], "group", scatter_dimension=0, tiled=True),
        lax.psum_scatter(grads[1], "group", scatter_dimension=0, tiled=True),
        lax.psum_scatter(grads[2], "group", scatter_dimension=0, tiled=True),
        lax.psum_scatter(grads[3], "group", scatter_dimension=0, tiled=True),
        lax.psum_scatter(grads[4], "group", scatter_dimension=0, tiled=True),
        lax.psum_scatter(grads[5], "group", scatter_dimension=0, tiled=True),
        lax.psum_scatter(grads[6], "group", scatter_dimension=0, tiled=True),
        lax.psum_scatter(grads[7], "group", scatter_dimension=0, tiled=True),
        lax.psum_scatter(grads[8], "group", scatter_dimension=0, tiled=True),
        lax.psum_scatter(grads[9], "group", scatter_dimension=0, tiled=True),
        lax.psum_scatter(grads[10], "group", scatter_dimension=0, tiled=True),
        lax.psum_scatter(grads[11], "group", scatter_dimension=0, tiled=True),
    )
    summed = lax.psum(
        (
            owned[0],
            owned[1],
            owned[2],
            owned[3],
            owned[4],
            owned[5],
            owned[6],
            owned[7],
            owned[8],
            owned[9],
            owned[10],
            owned[11],
        ),
        "replica",
    )
    return (
        outputs,
        input_grad,
        summed[0],
        summed[1],
        summed[2],
        summed[3],
        summed[4],
        summed[5],
        summed[6],
        summed[7],
        summed[8],
        summed[9],
        summed[10],
        summed[11],
    )


def solution(mesh):
    return jax.shard_map(
        per_device,
        mesh=mesh,
        in_specs=(
            P(("group", "replica"), None, None),
            P(("group", "replica"), None),
            P(("group", "replica"), None, None),
            P("group"),
            P("group"),
            P("group", None),
            P("group"),
            P("group", None),
            P("group"),
            P("group"),
            P("group"),
            P("group", None),
            P("group"),
            P("group", None),
            P("group"),
        ),
        out_specs=(
            P(("group", "replica"), None, None),
            P(("group", "replica"), None, None),
            P("group"),
            P("group"),
            P("group", None),
            P("group"),
            P("group", None),
            P("group"),
            P("group"),
            P("group"),
            P("group", None),
            P("group"),
            P("group", None),
            P("group"),
        ),
        check_vma=False,
    )
```

profile of v0, /device:TPU:0, one launch (start us, length us, event | category | flops | bytes accessed | tf_op | source)
XLA Modules:
  0.0 2333.0 jit_solution(5948088002728456721)
XLA Ops:
  14.8 14.5 all-reduce.19
  30.1 81.4 %all-gather.5.cloned.1.call-done = bf16[1600,4800]{1,0:T(8,128)(2,1)} async-done(((bf16[400,4800]{1,0:T(8,128)(2,1)}), bf16[1600,4800]{1,0:T(8,128)(2,1)}) %all-gather.5.cloned.1.call-update) | async-done | bytes 15360016 | tf_op jit(solution)/shard_map/all_gather | solution.py:268
  111.5 13.2 fusion
  128.8 25.2 %all-gather.7.cloned.1.call-done = bf16[1600,1600]{1,0:T(8,128)(2,1)} async-done(((bf16[400,1600]{1,0:T(8,128)(2,1)}), bf16[1600,1600]{1,0:T(8,128)(2,1)}) %all-gather.7.cloned.1.call-update) | async-done | bytes 5120016 | tf_op jit(solution)/shard_map/all_gather | solution.py:270
  159.0 125.5 %all-gather.9.cloned.1.call-done = bf16[1600,6400]{1,0:T(8,128)(2,1)} async-done(((bf16[400,6400]{1,0:T(8,128)(2,1)}), bf16[1600,6400]{1,0:T(8,128)(2,1)}) %all-gather.9.cloned.1.call-update) | async-done | bytes 20480016 | tf_op jit(solution)/shard_map/all_gather | solution.py:274
  284.5 12.4 convolution_add_fusion
  296.9 122.5 %all-gather.11.cloned.1.call-done = bf16[6400,1600]{1,0:T(8,128)(2,1)} async-done(((bf16[1600,1600]{1,0:T(8,128)(2,1)}), bf16[6400,1600]{1,0:T(8,128)(2,1)}) %all-gather.11.cloned.1.call-update) | async-done | bytes 20480016 | tf_op jit(solution)/shard_map/all_gather | solution.py:276
  419.4 12.0 fusion.65
  431.4 12.7 multiply_reduce_fusion
  446.3 5.7 fusion.55
  460.4 15.0 fusion.39
  476.9 16.5 fusion.34
  494.4 18.8 fusion.42
  517.2 9.8 fusion.27
  527.1 10.5 reduce-scatter.7.cloned.1.call-done
  537.6 224.2 %reduce-scatter.5.cloned.1.call-done = f32[400,4800]{1,0:T(8,128)} async-done(((f32[1600,4800]{1,0:T(8,128)}), f32[400,4800]{1,0:T(8,128)}) %reduce-scatter.5.cloned.1.call-update) | async-done | bytes 7680016 | tf_op jit(solution)/shard_map/reduce_scatter | solution.py:298
  761.8 295.6 %reduce-scatter.9.cloned.1.call-done = f32[400,6400]{1,0:T(8,128)} async-done(((f32[1600,6400]{1,0:T(8,128)}), f32[400,6400]{1,0:T(8,128)}) %reduce-scatter.9.cloned.1.call-update) | async-done | bytes 10240016 | tf_op jit(solution)/shard_map/reduce_scatter | solution.py:304
  1057.4 289.3 %reduce-scatter.11.cloned.1.call-done = f32[1600,1600]{1,0:T(8,128)} async-done(((f32[6400,1600]{1,0:T(8,128)}), f32[1600,1600]{1,0:T(8,128)}) %reduce-scatter.11.cloned.1.call-update) | async-done | bytes 10240016 | tf_op jit(solution)/shard_map/reduce_scatter | solution.py:306
  1350.0 14.8 fusion.9
  1364.8 18.3 all-reduce.25.cloned.1.call-done
  1389.2 39.9 %all-reduce.16 = (f32[400]{0:T(512)}, f32[400]{0:T(512)}, f32[800]{0:T(1024)}, f32[400]{0:T(512)}, f32[400]{0:T(512)}, /*index=5*/f32[400]{0:T(512)}, f32[1600]{0:T(1024)}, f32[400]{0:T(512)}) all-reduce(f32[400]{0:T(512)S(1)} %dynamic-slice.9, f32[400]{0:T(512)S(1)} %dynamic-slice.11, ...), channel_id=1, replica_groups=mesh['group'=4,'replica'=8] {'replica'}, use_global_device_ids=true, to_apply=%region_13.14 | all-reduce | flops 4800 | bytes 38400 | tf_op jit(solution)/shard_map/psum | solution.py:309
  1429.2 874.7 %all-reduce.23.cloned.1.call-done = (f32[400,4800]{1,0:T(8,128)}, f32[400,1600]{1,0:T(8,128)}, f32[400,6400]{1,0:T(8,128)}, f32[1600,1600]{1,0:T(8,128)}) async-done(((f32[400,4800]{1,0:T(8,128)}, f32[400,1600]{1,0:T(8,128)}, f32[400,6400]{1,0:T(8,128)}, f32[1600,1600]{1,0:T(8,128)}), (f32[400,4800]{1,0:T(8,128)}, f32[400,1600]{1,0:T(8,128)}, f32[400,6400]{1,0:T(8,128)}, ...) | async-done | bytes 30720016 | tf_op jit(solution)/shard_map/psum | solution.py:309
  2303.9 7.1 copy.64
  2312.4 9.3 copy.66
  (142 shorter events, 45.4 us)
Async XLA Ops:
  7.2 104.3 %all-gather.5.cloned.1.call-start = ((), (), s32[]{:S(2)}) async-start(), calls=%async_computation.4 | async-start | bytes 19456000 | tf_op jit(solution)/shard_map/all_gather | solution.py:268
  7.9 146.1 %all-gather.7.cloned.1.call-start = ((), (), s32[]{:S(2)}) async-start(), calls=%async_computation.5 | async-start | bytes 6656000 | tf_op jit(solution)/shard_map/all_gather | solution.py:270
  8.7 275.9 %all-gather.9.cloned.1.call-start = ((), (), s32[]{:S(2)}) async-start(), calls=%async_computation.6 | async-start | bytes 25600000 | tf_op jit(solution)/shard_map/all_gather | solution.py:274
  9.5 4.3 copy-start.23
  9.5 4.5 copy-start.24
  9.5 4.8 copy-start.18
  9.5 5.0 copy-start.15
  9.5 20.0 copy-start
  9.5 20.5 copy-start.16
  9.5 409.9 %all-gather.11.cloned.1.call-start = ((), (), s32[]{:S(2)}) async-start(), calls=%async_computation.7 | async-start | bytes 26624000 | tf_op jit(solution)/shard_map/all_gather | solution.py:276
  10.1 527.5 %reduce-scatter.7.cloned.1.call-start = ((), (), s32[]{:S(2)}) async-start(), calls=%async_computation.9 | async-start | bytes 13312000 | tf_op jit(solution)/shard_map/reduce_scatter | solution.py:300
  431.4 12.7 copy-start.3
  431.4 12.7 copy-start.13
  452.0 309.8 %reduce-scatter.5.cloned.1.call-start = ((), (), s32[]{:S(2)}) async-start(), calls=%async_computation.8 | async-start | bytes 38912000 | tf_op jit(solution)/shard_map/reduce_scatter | solution.py:298
  452.3 4.4 copy-start.11
  452.3 4.6 copy-start.10
  475.4 582.0 %reduce-scatter.9.cloned.1.call-start = ((), (), s32[]{:S(2)}) async-start(), calls=%async_computation.10 | async-start | bytes 51200000 | tf_op jit(solution)/shard_map/reduce_scatter | solution.py:304
  493.4 853.3 %reduce-scatter.11.cloned.1.call-start = ((), (), s32[]{:S(2)}) async-start(), calls=%async_computation.11 | async-start | bytes 53248000 | tf_op jit(solution)/shard_map/reduce_scatter | solution.py:306
  513.2 869.8 %all-reduce.25.cloned.1.call-start = ((), (), s32[]{:S(2)}) async-start(), calls=%async_computation.13 | async-start | bytes 188416
  527.0 1776.8 %all-reduce.23.cloned.1.call-start = ((), (), s32[]{:S(2)}) async-start(), calls=%async_computation.12 | async-start | bytes 62668800 | tf_op jit(solution)/shard_map/psum | solution.py:309
  2303.9 7.1 copy-start.12
  2310.9 10.8 slice-start
  2312.4 9.3 slice-start.1
  2312.4 9.3 slice-start.2
  (14 other events, 28.4 us)
Sparse Core Ops, SparseCore 0:
  9.5 101.8 all-gather.4
  113.0 40.9 all-gather.6
  155.6 128.8 all-gather.8
  285.9 133.3 all-gather.10
  452.1 85.4 reduce-scatter.6
  540.1 221.6 reduce-scatter.4
  764.4 292.9 reduce-scatter.8
  1060.0 286.6 reduce-scatter.10
  1350.7 32.3 all-reduce.24
  1387.8 916.0 all-reduce.22
where the time goes:
time: 2340 us; the launch traced here: 2330 us
  waiting for transfers between devices  2070 us (88%)
  matrix products  146 us (6%)
  blocking collectives  54.4 us (2%)
  local copies, waits for them, and re-layouts  36.2 us (2%)
    psum x1, waiting for transfers between devices, per_device(): lax.psum((owned[0], owned[1], owned[2], owned[3], owned[4], owned[5], own...  875 us
    reduce_scatter x1, waiting for transfers between devices, per_device(): lax.psum_scatter(grads[8], 'group', scatter_dimension=0, tiled=True)  296 us
    reduce_scatter x1, waiting for transfers between devices, per_device(): lax.psum_scatter(grads[10], 'group', scatter_dimension=0, tiled=True)  289 us
    reduce_scatter x1, waiting for transfers between devices, per_device(): lax.psum_scatter(grads[2], 'group', scatter_dimension=0, tiled=True)  224 us
    all_gather x1, waiting for transfers between devices, per_device(): lax.all_gather(w_fc, 'group', axis=0, tiled=True)  125 us
    all_gather x1, waiting for transfers between devices, per_device(): lax.all_gather(w_proj, 'group', axis=0, tiled=True)  122 us
    all_gather x1, waiting for transfers between devices, per_device(): lax.all_gather(w_qkv, 'group', axis=0, tiled=True)  81.4 us
    dot_general x4, matrix products, matmul_left(): lax.dot_general(left_side, right_side, (((0,), (0,)), ((), ())), preferre...  56 us
  transfers between devices with their start and end apart: 10, of which 10 were waited for; matrix products, arithmetic and copies ran while one was open for 6% of the time, Pallas kernels for 0%

commit v1 on v0

--- a/solution.py
+++ b/solution.py
@@ -7,6 +7,28 @@
 EPSILON = 1e-05
 GELU_SCALE = 0.7978845608028654
 CUBIC_TERM = 0.044715
+
+
+def laid_out(pieces, dim):
+    shape = list(pieces.shape[1:])
+    shape[dim] *= pieces.shape[0]
+    return jnp.moveaxis(pieces, 0, dim).reshape(shape)
+
+
+def ring_gather(shard, axis, dim):
+    size = lax.axis_size(axis)
+    pairs = [(i, (i + 1) % size) for i in range(size)]
+    back = [(b, a) for a, b in pairs]
+    lower, upper = ([], [])
+    for step in range(size - 1):
+        if step % 2 == 0:
+            lower.append(lax.ppermute(lower[-1] if lower else shard, axis, pairs))
+        else:
+            upper.append(lax.ppermute(upper[-1] if upper else shard, axis, back))
+    blocks = jnp.stack([*lower[::-1], shard, *upper])
+    shift = lax.axis_index(axis) - len(lower)
+    blocks = blocks[(jnp.arange(size) - shift) % size]
+    return laid_out(blocks, dim)
 
 
 def matmul_plain(left_side, right_side):
@@ -271,7 +293,7 @@
         lax.all_gather(bias_out, "group", axis=0, tiled=True),
         lax.all_gather(norm2_gain, "group", axis=0, tiled=True),
         lax.all_gather(norm2_bias, "group", axis=0, tiled=True),
-        lax.all_gather(w_fc, "group", axis=0, tiled=True),
+        ring_gather(w_fc, "group", 0),
         lax.all_gather(bias_fc, "group", axis=0, tiled=True),
         lax.all_gather(w_proj, "group", axis=0, tiled=True),
         lax.all_gather(bias_proj, "group", axis=0, tiled=True),

time: 2340 us -> 2450 us (1.047)
  blocking collectives: 54.4 us -> 168 us
  waiting for transfers between devices: 2070 us -> 1990 us
  other arithmetic: 6.75 us -> 40.1 us
  local copies, waits for them, and re-layouts: 36.2 us -> 63.4 us
    ppermute x0 -> x3, waiting for transfers between devices: none -> 192 us  [the longest x2 192 us: ring_gather(): lower.append(lax.ppermute(lower[-1] if lower else shard, axis, pairs))]
    all_gather x1, waiting for transfers between devices: 122 us -> 0.01 us  [per_device(): lax.all_gather(w_proj, 'group', axis=0, tiled=True)]
    unnamed x1, blocking collectives: 14.5 us -> 129 us
    all_gather x1, waiting for transfers between devices: 81.4 us -> 0.02 us  [per_device(): lax.all_gather(w_qkv, 'group', axis=0, tiled=True)]
    all_gather x1, waiting for transfers between devices: 125 us -> 86 us  [per_device(): lax.all_gather(w_fc, 'group', axis=0, tiled=True)]
    gather x0 -> x4, local copies, waits for them, and re-layouts: none -> 26.5 us  [ring_gather(): blocks = blocks[(jnp.arange(size) - shift) % size]]
    all_gather x1, waiting for transfers between devices: 25.2 us -> 0.01 us  [per_device(): lax.all_gather(w_out, 'group', axis=0, tiled=True)]
  transfers between devices with their start and end apart: 10 -> 13, of which waited for: 10 -> 8; matrix products, arithmetic and copies ran while one was open for 6% -> 8% of each run, Pallas kernels for 0% -> 0%
where the time goes in v1:
time: 2450 us; the launch traced here: 2440 us
  waiting for transfers between devices  1990 us (81%)
  blocking collectives  168 us (7%)
  matrix products  151 us (6%)
  local copies, waits for them, and re-layouts  63.4 us (3%)
  other arithmetic  40.1 us (2%)
    psum x1, waiting for transfers between devices, per_device(): lax.psum((owned[0], owned[1], owned[2], owned[3], owned[4], owned[5], own...  875 us
    reduce_scatter x1, waiting for transfers between devices, per_device(): lax.psum_scatter(grads[8], 'group', scatter_dimension=0, tiled=True)  296 us
    reduce_scatter x1, waiting for transfers between devices, per_device(): lax.psum_scatter(grads[10], 'group', scatter_dimension=0, tiled=True)  289 us
    reduce_scatter x1, waiting for transfers between devices, per_device(): lax.psum_scatter(grads[2], 'group', scatter_dimension=0, tiled=True)  224 us
    ppermute x2, waiting for transfers between devices, ring_gather(): lower.append(lax.ppermute(lower[-1] if lower else shard, axis, pairs))  192 us
    unnamed x1, blocking collectives  129 us
    all_gather x1, waiting for transfers between devices, per_device(): lax.all_gather(w_fc, 'group', axis=0, tiled=True)  86 us
    dot_general x4, matrix products, matmul_left(): lax.dot_general(left_side, right_side, (((0,), (0,)), ((), ())), preferre...  56.4 us
  transfers between devices with their start and end apart: 13, of which 8 were waited for; matrix products, arithmetic and copies ran while one was open for 8% of the time, Pallas kernels for 0%

profile of v1, /device:TPU:0, one launch (start us, length us, event | category | flops | bytes accessed | tf_op | source)
XLA Modules:
  0.0 2441.6 jit_solution(11339359754468329954)
XLA Ops:
  12.7 192.0 %collective-permute-done = bf16[400,6400]{1,0:T(8,128)(2,1)} collective-permute-done((bf16[400,6400]{1,0:T(8,128)(2,1)}, bf16[400,6400]{1,0:T(8,128)(2,1)}, u32[]{:S(2)}, u32[]{:S(2)}) %collective-permute-start) | collective-permute-done | bytes 5120032 | tf_op jit(solution)/shard_map/ppermute | solution.py:25
  213.7 128.5 %all-reduce.19 = (bf16[3200]{0:T(1024)(128)(2,1)S(1)}, bf16[1600]{0:T(1024)(128)(2,1)S(1)}, bf16[1600]{0:T(1024)(128)(2,1)S(1)}, bf16[1600]{0:T(1024)(128)(2,1)S...) all-reduce(bf16[3200]{0:T(1024)(128)(2,1)S(1)} %dynamic-update-slic, ...), channel_id=1, replica_groups=mesh['group'=4,'replica'=8] {'group'}, use_global_device_ids=true, to_apply=%add.2 | all-reduce | flops 19200 | bytes 76800
  356.4 10.0 pad_maximum_fusion
  371.9 7.2 gather_fusion.1
  379.1 7.2 gather_fusion
  386.3 16.8 pad_maximum_fusion.1
  403.1 13.4 fusion
  427.0 14.2 convolution_add_fusion
  441.2 13.1 fusion.68
  454.2 86.0 %all-gather.11.cloned.1.call-done = bf16[1600,6400]{1,0:T(8,128)(2,1)} async-done(((bf16[400,6400]{1,0:T(8,128)(2,1)}), bf16[1600,6400]{1,0:T(8,128)(2,1)}) %all-gather.11.cloned.1.call-update) | async-done | bytes 20480016 | tf_op jit(solution)/shard_map/all_gather | solution.py:311
  540.2 12.6 multiply_reduce_fusion
  569.3 14.9 fusion.39
  585.2 19.0 fusion.42
  605.6 16.8 fusion.34
  626.4 9.8 fusion.27
  636.2 10.1 reduce-scatter.7.cloned.1.call-done
  646.3 224.2 %reduce-scatter.5.cloned.1.call-done = f32[400,4800]{1,0:T(8,128)} async-done(((f32[1600,4800]{1,0:T(8,128)}), f32[400,4800]{1,0:T(8,128)}) %reduce-scatter.5.cloned.1.call-update) | async-done | bytes 7680016 | tf_op jit(solution)/shard_map/reduce_scatter | solution.py:320
  870.5 289.3 %reduce-scatter.11.cloned.1.call-done = f32[1600,1600]{1,0:T(8,128)} async-done(((f32[6400,1600]{1,0:T(8,128)}), f32[1600,1600]{1,0:T(8,128)}) %reduce-scatter.11.cloned.1.call-update) | async-done | bytes 10240016 | tf_op jit(solution)/shard_map/reduce_scatter | solution.py:328
  1159.8 295.6 %reduce-scatter.9.cloned.1.call-done = f32[400,6400]{1,0:T(8,128)} async-done(((f32[1600,6400]{1,0:T(8,128)}), f32[400,6400]{1,0:T(8,128)}) %reduce-scatter.9.cloned.1.call-update) | async-done | bytes 10240016 | tf_op jit(solution)/shard_map/reduce_scatter | solution.py:326
  1459.2 14.8 fusion.9
  1474.0 17.7 all-reduce.25.cloned.1.call-done
  1497.9 39.9 %all-reduce.16 = (f32[400]{0:T(512)}, f32[400]{0:T(512)}, f32[800]{0:T(1024)}, f32[400]{0:T(512)}, f32[400]{0:T(512)}, /*index=5*/f32[400]{0:T(512)}, f32[1600]{0:T(1024)}, f32[400]{0:T(512)}) all-reduce(f32[400]{0:T(512)S(1)} %dynamic-slice.9, f32[400]{0:T(512)S(1)} %dynamic-slice.11, ...), channel_id=1, replica_groups=mesh['group'=4,'replica'=8] {'replica'}, use_global_device_ids=true, to_apply=%region_13.14 | all-reduce | flops 4800 | bytes 38400 | tf_op jit(solution)/shard_map/psum | solution.py:331
  1537.8 874.7 %all-reduce.23.cloned.1.call-done = (f32[400,4800]{1,0:T(8,128)}, f32[400,1600]{1,0:T(8,128)}, f32[400,6400]{1,0:T(8,128)}, f32[1600,1600]{1,0:T(8,128)}) async-done(((f32[400,4800]{1,0:T(8,128)}, f32[400,1600]{1,0:T(8,128)}, f32[400,6400]{1,0:T(8,128)}, f32[1600,1600]{1,0:T(8,128)}), (f32[400,4800]{1,0:T(8,128)}, f32[400,1600]{1,0:T(8,128)}, f32[400,6400]{1,0:T(8,128)}, ...) | async-done | bytes 30720016 | tf_op jit(solution)/shard_map/psum | solution.py:331
  2421.1 9.3 copy.66
  (157 shorter events, 86.1 us)
Async XLA Ops:
  7.2 395.9 %all-gather.5.cloned.1.call-start = ((), (), s32[]{:S(2)}) async-start(), calls=%async_computation.4 | async-start | bytes 19456000 | tf_op jit(solution)/shard_map/all_gather | solution.py:290
  7.9 413.0 %all-gather.7.cloned.1.call-start = ((), (), s32[]{:S(2)}) async-start(), calls=%async_computation.5 | async-start | bytes 6656000 | tf_op jit(solution)/shard_map/all_gather | solution.py:292
  8.7 432.5 %all-gather.9.cloned.1.call-start = ((), (), s32[]{:S(2)}) async-start(), calls=%async_computation.6 | async-start | bytes 26624000 | tf_op jit(solution)/shard_map/all_gather | solution.py:298
  9.4 199.7 %copy-start.17 = (u32[32]{0:T(128)S(1)}, u32[32]{0:T(128)}, u32[]{:S(2)}) copy-start(u32[32]{0:T(128)} %constant.61) | copy-start | bytes 388
  9.4 202.2 %copy-start.19 = (bf16[400]{0:T(512)(128)(2,1)S(1)}, bf16[400]{0:T(512)(128)(2,1)}, u32[]{:S(2)}) copy-start(bf16[400]{0:T(512)(128)(2,1)} %param.19) | copy-start | bytes 2404
  9.4 202.5 %copy-start.20 = (bf16[400]{0:T(512)(128)(2,1)S(1)}, bf16[400]{0:T(512)(128)(2,1)}, u32[]{:S(2)}) copy-start(bf16[400]{0:T(512)(128)(2,1)} %param.18) | copy-start | bytes 2404
  9.4 202.7 %copy-start.21 = (bf16[400]{0:T(512)(128)(2,1)S(1)}, bf16[400]{0:T(512)(128)(2,1)}, u32[]{:S(2)}) copy-start(bf16[400]{0:T(512)(128)(2,1)} %param.23) | copy-start | bytes 2404
  9.4 203.0 %copy-start.22 = (bf16[400]{0:T(512)(128)(2,1)S(1)}, bf16[400]{0:T(512)(128)(2,1)}, u32[]{:S(2)}) copy-start(bf16[400]{0:T(512)(128)(2,1)} %param.29) | copy-start | bytes 2404
  9.5 203.2 %copy-start.23 = (bf16[400]{0:T(512)(128)(2,1)S(1)}, bf16[400]{0:T(512)(128)(2,1)}, u32[]{:S(2)}) copy-start(bf16[400]{0:T(512)(128)(2,1)} %param.25) | copy-start | bytes 2404
  9.5 203.5 %copy-start.24 = (bf16[400]{0:T(512)(128)(2,1)S(1)}, bf16[400]{0:T(512)(128)(2,1)}, u32[]{:S(2)}) copy-start(bf16[400]{0:T(512)(128)(2,1)} %param.24) | copy-start | bytes 2404
  9.5 203.7 %copy-start.18 = (bf16[800]{0:T(1024)(128)(2,1)S(1)}, bf16[800]{0:T(1024)(128)(2,1)}, u32[]{:S(2)}) copy-start(bf16[800]{0:T(1024)(128)(2,1)} %param.21) | copy-start | bytes 4804
  9.5 204.0 %copy-start.15 = (bf16[1600]{0:T(1024)(128)(2,1)S(1)}, bf16[1600]{0:T(1024)(128)(2,1)}, u32[]{:S(2)}) copy-start(bf16[1600]{0:T(1024)(128)(2,1)} %param.27) | copy-start | bytes 9604
  9.5 333.0 %copy-start = (bf16[1,128,1600]{1,2,0:T(8,128)(2,1)S(1)}, bf16[1,128,1600]{1,2,0:T(8,128)(2,1)}, u32[]{:S(2)}) copy-start(bf16[1,128,1600]{1,2,0:T(8,128)(2,1)} %param.15) | copy-start | bytes 1228804
  9.5 333.5 %copy-start.16 = (s32[1,128]{1,0:T(1,128)S(1)}, s32[1,128]{1,0:T(1,128)}, u32[]{:S(2)}) copy-start(s32[1,128]{1,0:T(1,128)} %param.16) | copy-start | bytes 1540
  9.5 530.7 %all-gather.11.cloned.1.call-start = ((), (), s32[]{:S(2)}) async-start(), calls=%async_computation.7 | async-start | bytes 25600000 | tf_op jit(solution)/shard_map/all_gather | solution.py:311
  10.1 636.2 %reduce-scatter.7.cloned.1.call-start = ((), (), s32[]{:S(2)}) async-start(), calls=%async_computation.9 | async-start | bytes 13312000 | tf_op jit(solution)/shard_map/reduce_scatter | solution.py:322
  10.1 194.6 %collective-permute-start = (bf16[400,6400]{1,0:T(8,128)(2,1)}, bf16[400,6400]{1,0:T(8,128)(2,1)}, u32[]{:S(2)}, u32[]{:S(2)}) collective-permute-start(bf16[400,6400]{1,0:T(8,128)(2,1)} %param.26), channel_id=1, source_target_pairs={{0,8},{8,16},{16,24},{24,0},{1,9},{9,17},{17,25},{25,1},{2,10},{10... | collective-permute-start | bytes 15360008 | tf_op jit(solution)/shard_map/ppermute | solution.py:25
  10.7 332.4 %collective-permute-start.2 = (bf16[400,6400]{1,0:T(8,128)(2,1)}, bf16[400,6400]{1,0:T(8,128)(2,1)}, u32[]{:S(2)}, u32[]{:S(2)}) collective-permute-start(bf16[400,6400]{1,0:T(8,128)(2,1)} %param.26), channel_id=1, source_target_pairs={{8,0},{16,8},{24,16},{0,24},{9,1},{17,9},{25,17},{1,25},{10,2},{18... | collective-permute-start | bytes 15360008 | tf_op jit(solution)/shard_map/ppermute | solution.py:27
  204.7 138.4 %collective-permute-start.1 = (bf16[400,6400]{1,0:T(8,128)(2,1)}, bf16[400,6400]{1,0:T(8,128)(2,1)}, u32[]{:S(2)}, u32[]{:S(2)}) collective-permute-start(bf16[400,6400]{1,0:T(8,128)(2,1)} %collective-permute-done), channel_id=1, source_target_pairs={{0,8},{8,16},{16,24},{24,0},{1,9},{9,17},{17,25},{25,1},{2,10},{10... | collective-permute-start | bytes 15360008 | tf_op jit(solution)/shard_map/ppermute | solution.py:25
  560.7 309.8 %reduce-scatter.5.cloned.1.call-start = ((), (), s32[]{:S(2)}) async-start(), calls=%async_computation.8 | async-start | bytes 38912000 | tf_op jit(solution)/shard_map/reduce_scatter | solution.py:320
  584.2 575.6 %reduce-scatter.11.cloned.1.call-start = ((), (), s32[]{:S(2)}) async-start(), calls=%async_computation.11 | async-start | bytes 53248000 | tf_op jit(solution)/shard_map/reduce_scatter | solution.py:328
  604.2 851.2 %reduce-scatter.9.cloned.1.call-start = ((), (), s32[]{:S(2)}) async-start(), calls=%async_computation.10 | async-start | bytes 51200000 | tf_op jit(solution)/shard_map/reduce_scatter | solution.py:326
  622.5 869.3 %all-reduce.25.cloned.1.call-start = ((), (), s32[]{:S(2)}) async-start(), calls=%async_computation.13 | async-start | bytes 188416
  636.1 1776.4 %all-reduce.23.cloned.1.call-start = ((), (), s32[]{:S(2)}) async-start(), calls=%async_computation.12 | async-start | bytes 62668800 | tf_op jit(solution)/shard_map/psum | solution.py:331
  (17 other events, 72.3 us)
Sparse Core Ops, SparseCore 0:
  9.5 185.2 all-gather.4
  196.4 55.2 all-gather.6
  253.2 154.5 all-gather.8
  409.3 130.8 all-gather.10
  560.8 85.4 reduce-scatter.6
  648.8 221.6 reduce-scatter.4
  873.1 286.6 reduce-scatter.10
  1162.4 292.9 reduce-scatter.8
  1459.4 32.3 all-reduce.24
  1496.4 916.0 all-reduce.22
